TPU v7x, 64 devices: a 2x2x8 block of a 4x4x8 slice. The times are simulated.
64 devices in a mesh: rep: 4 (over x, y), dp: 16 (over z, core).
Axes of the slice: x: 2, y: 2, z: 8, core: 2. Of those that a mesh axis runs over, the one named last changes fastest.
The devices are a block of a 4x4x8 slice.
Arguments:
- a: bfloat16 [64, 4, 4096, 896], P(('rep', 'dp')), parts along dimension 0
- g: bfloat16 [64, 4, 4096, 2304], P(('rep', 'dp')), parts along dimension 0
Outputs:
- output: bfloat16 [16, 896, 2304], P('rep'), parts along dimension 0
There are 4 independent parts. A program takes and returns all parts, laid end to end along the dimension named above; each array names one.
All inputs are finite; a program needn't handle non-finite values.
Results may differ from a plain program's by a relative error of at most 0.012.
Values are sent between devices in bfloat16 or wider.
A program may use at most 768 MiB of HBM per device.

v0:
```python
import jax
import jax.numpy as jnp


def solution(mesh):
    groups = mesh.shape["rep"]

    def step(a, g):
        a, g = (t.reshape(groups, -1, *t.shape[1:]) for t in (a, g))
        sums = jnp.einsum("rsntd,rsntf->rndf", a, g, preferred_element_type=jnp.float32)
        return sums.astype(jnp.bfloat16).reshape(-1, *sums.shape[2:])

    return step
```

profile of v0, /device:TPU:30, one launch (start us, length us, event | category | flops | bytes accessed | tf_op | source)
XLA Modules:
  0.0 445.8 jit_solution(2314249322955101246)
XLA Ops:
  0.0 78.6 %fusion.3 = f32[1,4,896,2304]{3,2,1,0:T(8,128)} fusion(bf16[1,4,4096,2304]{3,2,1,0:T(8,128)(2,1)} %param.1, bf16[1,4,4096,896]{3,2,1,0:T(8,128)(2,1)} %param), kind=kOutput, calls=%fused_computation.3 | convolution fusion | flops 67645734912 | bytes 137887744 | tf_op jit(solution)/rsntd,rsntf->rndf/dot_general | solution.py:10
  78.6 367.2 %all-reduce.2 = bf16[1,4,896,2304]{3,2,1,0:T(8,128)(2,1)} all-reduce(f32[1,4,896,2304]{3,2,1,0:T(8,128)} %fusion.3), channel_id=1, replica_groups=[4,16]<=[64], use_global_device_ids=true, to_apply=%add.clone | all-reduce | flops 8257536 | bytes 49545216 | tf_op jit(solution)/rsntd,rsntf->rndf/dot_general | solution.py:10
where the time goes:
time: 446 us
  blocking collectives  367 us (82%)
  matrix products  78.6 us (18%)
    dot_general x1, blocking collectives, step(): jnp.einsum('rsntd,rsntf->rndf', a, g, preferred_element_type=jnp.float32)  367 us
    dot_general x1, matrix products, step(): jnp.einsum('rsntd,rsntf->rndf', a, g, preferred_element_type=jnp.float32)  78.6 us

commit v1 on v0

v1 whole, which is shorter than its diff:
```python
import functools

import jax
import jax.numpy as jnp
from jax import lax
from jax.experimental import pallas as pl
from jax.experimental.pallas import tpu as pltpu
from jax.sharding import PartitionSpec as P

WIDTH = 256
LAG = 3
SLOTS = 4
MESH = pl.DeviceIdType.MESH


def kernel(
    chips, a, g, total,
    a_buf, g_buf, term, x_out, x_in,
    a_sem, g_sem, xs_sem, xr_sem, rs_send, rs_recv, ag_send, ag_recv, d2_send, d2_recv, free_sem,
):
    n_mat, ff = g.shape[1], g.shape[3]
    d_rows = a.shape[3]
    half = d_rows // 2
    cols = ff // WIDTH
    tiles = n_mat * cols // 2
    me = lax.axis_index("dp")
    z, core = me // 2, lax.rem(me, 2)
    partner = {"dp": z * 2 + 1 - core}

    def ring(d):
        place = jnp.where(d == 0, z, chips - 1 - z)
        to = lax.rem(z + jnp.where(d == 0, 1, chips - 1), chips)
        return place, {"dp": to * 2 + core}

    def start_of(b):
        return tiles * b // chips

    def tile_of(d, q):
        place, _ = ring(d)
        u = lax.rem(start_of(place) + 2 * tiles - 1 - q, tiles)
        return d * tiles + u

    def size_of(b):
        return start_of(b + 1) - start_of(b)

    def place_of(t):
        return t // cols, pl.ds(pl.multiple_of(lax.rem(t, cols) * WIDTH, WIDTH), WIDTH)

    def a_copy(n):
        return pltpu.make_async_copy(a.at[0, n], a_buf.at[n], a_sem.at[n])

    def g_copy(d, q):
        n, c = place_of(tile_of(d, q))
        slot = lax.rem(q, 2)
        return pltpu.make_async_copy(g.at[0, n, :, c], g_buf.at[d, slot], g_sem.at[d, slot])

    def x_copy(t):
        slot = lax.rem(t, SLOTS)
        return pltpu.make_async_remote_copy(
            src_ref=x_out.at[slot], dst_ref=x_in.at[slot], send_sem=xs_sem.at[slot], recv_sem=xr_sem.at[slot],
            device_id=partner, device_id_type=MESH)

    def move(t, to, send, recv):
        return pltpu.make_async_remote_copy(
            src_ref=total.at[t, core], dst_ref=total.at[t, core], send_sem=send.at[t], recv_sem=recv.at[t],
            device_id=to, device_id_type=MESH)

    def from_partner(t):
        return pltpu.make_async_remote_copy(
            src_ref=total.at[t, 1 - core], dst_ref=total.at[t, 1 - core], send_sem=d2_send.at[t], recv_sem=d2_recv.at[t],
            device_id=partner, device_id_type=MESH)

    def give(d, q):
        move(tile_of(d, q), ring(d)[1], rs_send, rs_recv).wait_send()
        pl.semaphore_signal(free_sem.at[d], inc=1, device_id=ring(1 - d)[1], device_id_type=MESH)

    first = [tile_of(d, 0) // cols for d in range(2)]
    other = [4 * d + 1 - first[d] for d in range(2)]
    for d in range(2):
        g_copy(d, 0).start()
        a_copy(first[d]).start()
    for d in range(2):
        g_copy(d, 1).start()
    for d in range(2):
        a_copy(other[d]).start()

    barrier = pltpu.get_barrier_semaphore()
    for to in (ring(0)[1], ring(1)[1], partner):
        pl.semaphore_signal(barrier, inc=1, device_id=to, device_id_type=MESH)
    pl.semaphore_wait(barrier, 3)

    def compute(d, q):
        t = tile_of(d, q)
        n = t // cols
        slot = lax.rem(q, 2)
        x_slot = lax.rem(2 * q + d, SLOTS)
        g_copy(d, q).wait()
        start = tile_of(d, 0)

        @pl.when(q == 0)
        def _():
            a_copy(start // cols).wait()

        @pl.when(q == lax.rem(start, cols) + 1)
        def _():
            a_copy(4 * d + 1 - start // cols).wait()

        product = lax.dot_general(
            a_buf[n], g_buf[d, slot], (((0,), (0,)), ((), ())), preferred_element_type=jnp.float32)
        term[d, 0] = product[:half]
        term[d, 1] = product[half:]
        x_out[x_slot] = term[d, 1 - core].astype(jnp.bfloat16)
        x_copy(2 * q + d).start()

        @pl.when(q + 2 < tiles)
        def _():
            g_copy(d, q + 2).start()

    def reduce(d, q):
        place, to = ring(d)
        t = tile_of(d, q)
        before = lax.rem(place + chips - 1, chips)
        x_copy(2 * q + d).wait()
        term[d, core] += x_in[lax.rem(2 * q + d, SLOTS)].astype(jnp.float32)

        @pl.when(q >= size_of(before))
        def _():
            move(t, to, rs_send, rs_recv).wait_recv()
            term[d, core] += total[t, core].astype(jnp.float32)

        total[t, core] = term[d, core].astype(jnp.bfloat16)
        last = q >= tiles - size_of(place)

        @pl.when(jnp.logical_not(last))
        def _():
            move(t, to, rs_send, rs_recv).start()

        @pl.when(jnp.logical_and(q >= LAG, q - LAG < tiles - size_of(place)))
        def _():
            give(d, q - LAG)

        @pl.when(last)
        def _():
            pl.semaphore_wait(free_sem.at[d], 1)
            move(t, to, ag_send, ag_recv).start()
            move(t, partner, d2_send, d2_recv).start()

    def step(t, _):
        compute(lax.rem(t, 2), t // 2)

        @pl.when(t > 0)
        def _():
            reduce(lax.rem(t - 1, 2), (t - 1) // 2)

        return 0

    lax.fori_loop(0, 2 * tiles, step, 0)
    reduce(1, tiles - 1)

    for d in range(2):
        for i in range(LAG):
            @pl.when(tiles - LAG + i < tiles - size_of(ring(d)[0]))
            def _():
                give(d, tiles - LAG + i)

    def gather(r, _):
        for d in range(2):
            place, to = ring(d)
            after = lax.rem(place + 1, chips)
            count = tiles - size_of(place)
            t = tile_of(d, r)

            @pl.when(r < count)
            def _():
                move(t, to, ag_send, ag_recv).wait_recv()

                @pl.when(r < count - size_of(after))
                def _():
                    pl.semaphore_wait(free_sem.at[d], 1)
                    move(t, to, ag_send, ag_recv).start()

                move(t, partner, d2_send, d2_recv).start()

        for d in range(2):
            from_partner(tile_of(d, r + tiles - 1)).wait_recv()
        return 0

    lax.fori_loop(0, tiles, gather, 0)

    def drain(q, _):
        for d in range(2):
            place, to = ring(d)
            after = lax.rem(place + 1, chips)
            count = tiles - size_of(place)
            t = tile_of(d, q)
            move(t, partner, d2_send, d2_recv).wait_send()

            @pl.when(jnp.logical_or(q < count - size_of(after), q >= count))
            def _():
                move(t, to, ag_send, ag_recv).wait_send()
        return 0

    lax.fori_loop(0, tiles, drain, 0)


def writer(sums, out, sem):
    tiles, _, half, _ = sums.shape
    cols = tiles // out.shape[0]

    def write(i, _):
        t, h = i // 2, lax.rem(i, 2)
        rows = pl.ds(pl.multiple_of(h * half, 8), half)
        columns = pl.ds(pl.multiple_of(lax.rem(t, cols) * WIDTH, WIDTH), WIDTH)
        pltpu.make_async_copy(sums.at[t, h], out.at[t // cols, rows, columns], sem).start()
        return 0

    lax.fori_loop(0, 2 * tiles, write, 0)
    pltpu.make_async_copy(out, out, sem).wait()


def sums(chips, a, g):
    _, n_mat, tokens, d_rows = a.shape
    ff = g.shape[-1]
    half = d_rows // 2
    tiles = n_mat * (ff // WIDTH)
    dma = pltpu.SemaphoreType.DMA
    total = pl.pallas_call(
        functools.partial(kernel, chips),
        out_shape=pltpu.VMEM((tiles, 2, half, WIDTH), jnp.bfloat16),
        in_specs=[pl.BlockSpec(memory_space=pl.ANY)] * 2,
        out_specs=pl.BlockSpec(memory_space=pltpu.VMEM),
        scratch_shapes=[
            pltpu.VMEM((n_mat, tokens, d_rows), jnp.bfloat16),
            pltpu.VMEM((2, 2, tokens, WIDTH), jnp.bfloat16),
            pltpu.VMEM((2, 2, half, WIDTH), jnp.float32),
            pltpu.VMEM((SLOTS, half, WIDTH), jnp.bfloat16),
            pltpu.VMEM((SLOTS, half, WIDTH), jnp.bfloat16),
            dma((n_mat,)), dma((2, 2)), dma((SLOTS,)), dma((SLOTS,)),
            dma((tiles,)), dma((tiles,)), dma((tiles,)), dma((tiles,)), dma((tiles,)), dma((tiles,)),
            pltpu.SemaphoreType.REGULAR((2,)),
        ],
        compiler_params=pltpu.CompilerParams(
            collective_id=0, has_side_effects=True, vmem_limit_bytes=46 << 20),
        name="sums",
    )(a, g)
    return pl.pallas_call(
        writer,
        out_shape=jax.ShapeDtypeStruct((n_mat, d_rows, ff), jnp.bfloat16),
        in_specs=[pl.BlockSpec(memory_space=pltpu.VMEM)],
        out_specs=pl.BlockSpec(memory_space=pl.ANY),
        scratch_shapes=[dma(())],
        compiler_params=pltpu.CompilerParams(vmem_limit_bytes=40 << 20),
        name="writer",
    )(pltpu.with_memory_space_constraint(total, pltpu.VMEM))


def solution(mesh):
    chips = mesh.shape["dp"] // 2
    return jax.shard_map(
        functools.partial(sums, chips), mesh=mesh,
        in_specs=(P(("rep", "dp")), P(("rep", "dp"))), out_specs=P("rep"), check_vma=False)
```

time: 446 us -> 182 us (0.41)
  the two profiles are of different devices: /device:TPU:30 before, /device:TPU:61 now
where the time goes in v1:
time: 182 us
  Pallas kernels  182 us (100%)
    pallas_call x1, Pallas kernels, sums(): pl.pallas_call(functools.partial(kernel, chips), out_shape=pltpu.VMEM((ti...  176 us
    pallas_call x1, Pallas kernels, sums(): pl.pallas_call(writer, out_shape=jax.ShapeDtypeStruct((n_mat, d_rows, ff)...  5.73 us

profile of v1, /device:TPU:61, one launch (start us, length us, event | category | flops | bytes accessed | tf_op | source)
XLA Modules:
  0.0 182.2 jit_solution(228045514237488085)
XLA Ops:
  0.0 176.5 %sums.1 = bf16[36,2,448,256]{3,2,1,0:T(8,128)(2,1)S(1)} custom-call(bf16[1,4,4096,896]{3,2,1,0:T(8,128)(2,1)} %a.1, bf16[1,4,4096,2304]{3,2,1,0:T(8,128)(2,1)} %g.1), custom_call_target="tpu_custom_call" | custom-call | tf_op jit(solution)/shard_map/sums/pallas_call | solution.py:227
  176.5 5.7 %writer.1 = bf16[4,896,2304]{2,1,0:T(8,128)(2,1)} custom-call(bf16[36,2,448,256]{3,2,1,0:T(8,128)(2,1)S(1)} %sums.1), custom_call_target="tpu_custom_call" | custom-call | tf_op jit(solution)/shard_map/writer/pallas_call | solution.py:246

commit v2 on v1

--- a/solution.py
+++ b/solution.py
@@ -16,7 +16,7 @@
 def kernel(
     chips, a, g, total,
     a_buf, g_buf, term, x_out, x_in,
-    a_sem, g_sem, xs_sem, xr_sem, rs_send, rs_recv, ag_send, ag_recv, d2_send, d2_recv, free_sem,
+    a_sem, g_sem, xs_sem, xr_sem, rs_send, ag_send, recv, swap_sem, free_sem,
 ):
     n_mat, ff = g.shape[1], g.shape[3]
     d_rows = a.shape[3]
@@ -60,34 +60,38 @@
             src_ref=x_out.at[slot], dst_ref=x_in.at[slot], send_sem=xs_sem.at[slot], recv_sem=xr_sem.at[slot],
             device_id=partner, device_id_type=MESH)
 
-    def move(t, to, send, recv):
+    def move(t, to, send):
         return pltpu.make_async_remote_copy(
-            src_ref=total.at[t, core], dst_ref=total.at[t, core], send_sem=send.at[t], recv_sem=recv.at[t],
+            src_ref=total.at[t, core], dst_ref=total.at[t, core], send_sem=send, recv_sem=recv.at[t],
             device_id=to, device_id_type=MESH)
 
-    def from_partner(t):
+    def running(d, q):
+        return move(tile_of(d, q), ring(d)[1], rs_send.at[d, lax.rem(q, LAG + 1)])
+
+    def final(d, t, s):
+        return move(t, ring(d)[1], ag_send.at[d, lax.rem(s, LAG + 1)])
+
+    def swap(t):
         return pltpu.make_async_remote_copy(
-            src_ref=total.at[t, 1 - core], dst_ref=total.at[t, 1 - core], send_sem=d2_send.at[t], recv_sem=d2_recv.at[t],
+            src_ref=total.at[t, core], dst_ref=total.at[t, core], send_sem=swap_sem.at[0], recv_sem=swap_sem.at[1],
             device_id=partner, device_id_type=MESH)
 
     def give(d, q):
-        move(tile_of(d, q), ring(d)[1], rs_send, rs_recv).wait_send()
+        running(d, q).wait_send()
         pl.semaphore_signal(free_sem.at[d], inc=1, device_id=ring(1 - d)[1], device_id_type=MESH)
 
-    first = [tile_of(d, 0) // cols for d in range(2)]
-    other = [4 * d + 1 - first[d] for d in range(2)]
-    for d in range(2):
-        g_copy(d, 0).start()
-        a_copy(first[d]).start()
-    for d in range(2):
-        g_copy(d, 1).start()
-    for d in range(2):
-        a_copy(other[d]).start()
+    g_copy(0, 0).start()
+    a_copy(tile_of(0, 0) // cols).start()
 
     barrier = pltpu.get_barrier_semaphore()
     for to in (ring(0)[1], ring(1)[1], partner):
         pl.semaphore_signal(barrier, inc=1, device_id=to, device_id_type=MESH)
     pl.semaphore_wait(barrier, 3)
+
+    g_copy(1, 0).start()
+    a_copy(tile_of(1, 0) // cols).start()
+    for d in range(2):
+        g_copy(d, 1).start()
 
     def compute(d, q):
         t = tile_of(d, q)
@@ -100,6 +104,7 @@
         @pl.when(q == 0)
         def _():
             a_copy(start // cols).wait()
+            a_copy(4 * d + 1 - start // cols).start()
 
         @pl.when(q == lax.rem(start, cols) + 1)
         def _():
@@ -107,9 +112,9 @@
 
         product = lax.dot_general(
             a_buf[n], g_buf[d, slot], (((0,), (0,)), ((), ())), preferred_element_type=jnp.float32)
-        term[d, 0] = product[:half]
-        term[d, 1] = product[half:]
-        x_out[x_slot] = term[d, 1 - core].astype(jnp.bfloat16)
+        low, high = product[:half], product[half:]
+        x_out[x_slot] = jnp.where(core == 0, high, low).astype(jnp.bfloat16)
+        term[d] = jnp.where(core == 0, low, high)
         x_copy(2 * q + d).start()
 
         @pl.when(q + 2 < tiles)
@@ -117,33 +122,35 @@
             g_copy(d, q + 2).start()
 
     def reduce(d, q):
-        place, to = ring(d)
+        place, _ = ring(d)
         t = tile_of(d, q)
         before = lax.rem(place + chips - 1, chips)
+        sent = tiles - size_of(place)
         x_copy(2 * q + d).wait()
-        term[d, core] += x_in[lax.rem(2 * q + d, SLOTS)].astype(jnp.float32)
+
+        @pl.when(q < size_of(before))
+        def _():
+            total[t, core] = (term[d] + x_in[lax.rem(2 * q + d, SLOTS)].astype(jnp.float32)).astype(jnp.bfloat16)
 
         @pl.when(q >= size_of(before))
         def _():
-            move(t, to, rs_send, rs_recv).wait_recv()
-            term[d, core] += total[t, core].astype(jnp.float32)
-
-        total[t, core] = term[d, core].astype(jnp.bfloat16)
-        last = q >= tiles - size_of(place)
-
-        @pl.when(jnp.logical_not(last))
-        def _():
-            move(t, to, rs_send, rs_recv).start()
-
-        @pl.when(jnp.logical_and(q >= LAG, q - LAG < tiles - size_of(place)))
+            running(d, q).wait_recv()
+            here = term[d] + x_in[lax.rem(2 * q + d, SLOTS)].astype(jnp.float32)
+            total[t, core] = (here + total[t, core].astype(jnp.float32)).astype(jnp.bfloat16)
+
+        @pl.when(q < sent)
+        def _():
+            running(d, q).start()
+
+        @pl.when(jnp.logical_and(q >= LAG, q - LAG < sent))
         def _():
             give(d, q - LAG)
 
-        @pl.when(last)
+        @pl.when(q >= sent)
         def _():
             pl.semaphore_wait(free_sem.at[d], 1)
-            move(t, to, ag_send, ag_recv).start()
-            move(t, partner, d2_send, d2_recv).start()
+            final(d, t, q - sent).start()
+            swap(t).start()
 
     def step(t, _):
         compute(lax.rem(t, 2), t // 2)
@@ -165,42 +172,34 @@
 
     def gather(r, _):
         for d in range(2):
-            place, to = ring(d)
-            after = lax.rem(place + 1, chips)
+            place, _ = ring(d)
             count = tiles - size_of(place)
             t = tile_of(d, r)
+            s = size_of(place) + r
 
             @pl.when(r < count)
             def _():
-                move(t, to, ag_send, ag_recv).wait_recv()
-
-                @pl.when(r < count - size_of(after))
+                final(d, t, s).wait_recv()
+
+                @pl.when(r < count - size_of(lax.rem(place + 1, chips)))
                 def _():
+                    @pl.when(s > LAG)
+                    def _():
+                        final(d, t, s).wait_send()
+
                     pl.semaphore_wait(free_sem.at[d], 1)
-                    move(t, to, ag_send, ag_recv).start()
-
-                move(t, partner, d2_send, d2_recv).start()
-
-        for d in range(2):
-            from_partner(tile_of(d, r + tiles - 1)).wait_recv()
+                    final(d, t, s).start()
+
+                swap(t).start()
+
         return 0
 
     lax.fori_loop(0, tiles, gather, 0)
 
-    def drain(q, _):
-        for d in range(2):
-            place, to = ring(d)
-            after = lax.rem(place + 1, chips)
-            count = tiles - size_of(place)
-            t = tile_of(d, q)
-            move(t, partner, d2_send, d2_recv).wait_send()
-
-            @pl.when(jnp.logical_or(q < count - size_of(after), q >= count))
-            def _():
-                move(t, to, ag_send, ag_recv).wait_send()
-        return 0
-
-    lax.fori_loop(0, tiles, drain, 0)
+    for d in range(2):
+        for i in range(LAG + 1):
+            final(d, 0, i).wait_send()
+    swap(slice(None)).wait()
 
 
 def writer(sums, out, sem):
@@ -232,11 +231,11 @@
         scratch_shapes=[
             pltpu.VMEM((n_mat, tokens, d_rows), jnp.bfloat16),
             pltpu.VMEM((2, 2, tokens, WIDTH), jnp.bfloat16),
-            pltpu.VMEM((2, 2, half, WIDTH), jnp.float32),
+            pltpu.VMEM((2, half, WIDTH), jnp.float32),
             pltpu.VMEM((SLOTS, half, WIDTH), jnp.bfloat16),
             pltpu.VMEM((SLOTS, half, WIDTH), jnp.bfloat16),
             dma((n_mat,)), dma((2, 2)), dma((SLOTS,)), dma((SLOTS,)),
-            dma((tiles,)), dma((tiles,)), dma((tiles,)), dma((tiles,)), dma((tiles,)), dma((tiles,)),
+            dma((2, LAG + 1)), dma((2, LAG + 1)), dma((tiles,)), dma((2,)),
             pltpu.SemaphoreType.REGULAR((2,)),
         ],
         compiler_params=pltpu.CompilerParams(

time: 182 us -> 180 us (0.989)
  the two profiles are of different devices: /device:TPU:61 before, /device:TPU:30 now
where the time goes in v2:
time: 180 us; the launch traced here: 177 us
  Pallas kernels  177 us (98%)
    pallas_call x1, Pallas kernels, sums(): pl.pallas_call(functools.partial(kernel, chips), out_shape=pltpu.VMEM((ti...  171 us
    pallas_call x1, Pallas kernels, sums(): pl.pallas_call(writer, out_shape=jax.ShapeDtypeStruct((n_mat, d_rows, ff)...  5.73 us

profile of v2, /device:TPU:30, one launch (start us, length us, event | category | flops | bytes accessed | tf_op | source)
XLA Modules:
  0.0 176.9 jit_solution(5936253161292282371)
XLA Ops:
  0.0 171.2 %sums.1 = bf16[36,2,448,256]{3,2,1,0:T(8,128)(2,1)S(1)} custom-call(bf16[1,4,4096,896]{3,2,1,0:T(8,128)(2,1)} %a.1, bf16[1,4,4096,2304]{3,2,1,0:T(8,128)(2,1)} %g.1), custom_call_target="tpu_custom_call" | custom-call | tf_op jit(solution)/shard_map/sums/pallas_call | solution.py:226
  171.2 5.7 %writer.1 = bf16[4,896,2304]{2,1,0:T(8,128)(2,1)} custom-call(bf16[36,2,448,256]{3,2,1,0:T(8,128)(2,1)S(1)} %sums.1), custom_call_target="tpu_custom_call" | custom-call | tf_op jit(solution)/shard_map/writer/pallas_call | solution.py:245
